TPU v7x, 32 devices: a whole 2x2x4 slice. The times are simulated.
32 devices in a mesh: gx: 2 (over y), gy: 8 (over z, core), gz: 2 (over x).
Axes of the slice: x: 2, y: 2, z: 4, core: 2. Of those that a mesh axis runs over, the one named last changes fastest.
Arguments:
- starting_kelvin: float32 [16, 32, 2048], P(None, 'gx', ('gy', 'gz')), may hold values from -6 to 6
- substance_label: int32 [16, 32, 2048], P(None, 'gx', ('gy', 'gz')), may hold values from 0 to 3
- voxel_source_patch: int32 [16, 32, 2048], P(None, 'gx', ('gy', 'gz')), may hold values from 0 to 15
- substance_traits: float32 [4, 4], replicated, may hold values from 0.5 to 2
- patch_source_intensity: float32 [16], replicated, may hold values from 0 to 8
Outputs:
- warmed_result: float32 [16, 32, 2048], P(None, 'gx', ('gy', 'gz'))
- solution: float32 [3, 16, 32, 2048], P(None, 'gz', 'gx', 'gy')
- residual: float32 [3, 16, 32, 2048], P(None, 'gz', 'gx', 'gy')
All inputs are finite; a program needn't handle non-finite values.
Results may differ from a plain program's by a relative error of at most 0.0029.
Values sent between devices are 32-bit elements; how exact they have to be, the bound alone decides.
A program may use at most 64 MiB of HBM per device.

v0:
```python
import jax
import jax.numpy as jnp
from jax import lax
from jax.sharding import PartitionSpec as P

ITERS = 3
time_step = 0.03
anchor_scale = 0.5
strain_gain = 2.0


def padded(value, sides, width):
    for axis, dim in sides:
        devices, length = (lax.axis_size(axis), value.shape[dim])
        up = [(i, (i + 1) % devices) for i in range(devices - 1)]
        down = [(j, i) for i, j in up]
        last = lax.slice_in_dim(value, length - width, length, axis=dim)
        initial = lax.slice_in_dim(value, 0, width, axis=dim)
        before = lax.ppermute(last, axis, up)
        after = lax.ppermute(initial, axis, down)
        value = jnp.concatenate([before, value, after], axis=dim)
    return value


def lookup(identity, table, count):
    summed = jnp.zeros(identity.shape, jnp.float32)
    for number in range(count):
        summed = summed + jnp.where(identity == number, table[number], jnp.float32(0.0))
    return summed


def conduct(own, other):
    return 2.0 * own * other / jnp.maximum(own + other, 0.25)


def heat_step(padded_temp, padded_cond, power, inverse_cap):
    centre = padded_temp[:, 1:-1, 1:-1]
    own = padded_cond[:, 1:-1, 1:-1]
    layers, rows, columns = centre.shape
    heat_flux = jnp.zeros_like(centre)
    for row_offset, column_offset in ((0, 1), (2, 1), (1, 0), (1, 2)):
        neighbour = padded_temp[
            :, row_offset : row_offset + rows, column_offset : column_offset + columns
        ]
        other = padded_cond[
            :, row_offset : row_offset + rows, column_offset : column_offset + columns
        ]
        heat_flux = heat_flux + conduct(own, other) * (neighbour - centre)
    vertical_temp = jnp.pad(centre, ((1, 1), (0, 0), (0, 0)))
    vertical_cond = jnp.pad(own, ((1, 1), (0, 0), (0, 0)))
    for layer_offset in (0, 2):
        other = vertical_cond[layer_offset : layer_offset + layers]
        neighbour = vertical_temp[layer_offset : layer_offset + layers]
        heat_flux = heat_flux + conduct(own, other) * (neighbour - centre)
    return centre + time_step * inverse_cap * (heat_flux + power)


def neighbour_offsets():
    listed = []
    for along_z in (-1, 0, 1):
        for along_x in (-1, 0, 1):
            for along_y in (-1, 0, 1):
                if along_z != 0 or along_x != 0 or along_y != 0:
                    listed.append((along_z, along_x, along_y))
    return listed


def apply_operator(field, padded_field, modulus, padded_modulus):
    layers, rows, columns = modulus.shape
    parts = [
        anchor_scale * modulus * field[0],
        anchor_scale * modulus * field[1],
        anchor_scale * modulus * field[2],
    ]
    for along_z, along_x, along_y in neighbour_offsets():
        length_sq = along_z * along_z + along_x * along_x + along_y * along_y
        window = (
            slice(1 + along_z, 1 + along_z + layers),
            slice(1 + along_x, 1 + along_x + rows),
            slice(1 + along_y, 1 + along_y + columns),
        )
        weight = 0.5 / length_sq * (modulus + padded_modulus[window])
        change = [field[index_c] - padded_field[index_c][window] for index_c in range(3)]
        projected = (along_z * change[0] + along_x * change[1] + along_y * change[2]) / length_sq
        for index_c, direction_part in enumerate((along_z, along_x, along_y)):
            parts[index_c] = parts[index_c] + weight * (
                0.5 * change[index_c] + direction_part * projected
            )
    return jnp.stack(parts)


def thermal_load(modulus, padded_modulus, strain, padded_strain):
    layers, rows, columns = modulus.shape
    parts = [jnp.zeros_like(modulus), jnp.zeros_like(modulus), jnp.zeros_like(modulus)]
    for along_z, along_x, along_y in neighbour_offsets():
        length_sq = along_z * along_z + along_x * along_x + along_y * along_y
        window = (
            slice(1 + along_z, 1 + along_z + layers),
            slice(1 + along_x, 1 + along_x + rows),
            slice(1 + along_y, 1 + along_y + columns),
        )
        weight = 0.5 / length_sq * (modulus + padded_modulus[window])
        pushing = weight * (0.5 * (strain + padded_strain[window]))
        for index_c, direction_part in enumerate((along_z, along_x, along_y)):
            if direction_part != 0:
                parts[index_c] = parts[index_c] - strain_gain * direction_part * pushing
    return jnp.stack(parts)


def two_products(residual, image):
    return lax.psum((jnp.sum(residual * residual), jnp.sum(residual * image)), ("gx", "gy", "gz"))


def per_device(
    starting_kelvin, substance_label, voxel_source_patch, substance_traits, patch_source_intensity
):
    count = substance_traits.shape[1]
    diffusive_coefficient = lookup(substance_label, substance_traits[0], count)
    inverse_cap = 1.0 / lookup(substance_label, substance_traits[1], count)
    power = lookup(voxel_source_patch, patch_source_intensity, patch_source_intensity.shape[0])
    padded_array = padded(
        jnp.stack([starting_kelvin, diffusive_coefficient]), (("gx", 2), (("gy", "gz"), 3)), 1
    )
    padded_cond = padded_array[1]
    warmed_result = heat_step(padded_array[0], padded_cond, power, inverse_cap)
    number = 0
    extended = padded(warmed_result, (("gx", 1), (("gy", "gz"), 2)), 1)
    warmed_result = heat_step(extended, padded_cond, power, inverse_cap)
    modulus = lookup(substance_label, substance_traits[2], count)
    strain = lookup(substance_label, substance_traits[3], count) * warmed_result
    fields = jnp.stack([modulus, strain])
    vertical_cycle = ((0, 0), (1, 1), (0, 0), (0, 0))
    padded_fields = jnp.pad(padded(fields, (("gx", 2), (("gy", "gz"), 3)), 1), vertical_cycle)

    def extend(field):
        return jnp.pad(padded(field, (("gx", 2), (("gy", "gz"), 3)), 1), vertical_cycle)

    modulus = fields[0]
    padded_modulus = padded_fields[0]
    load = thermal_load(modulus, padded_modulus, fields[1], padded_fields[1])

    def operate(field):
        return apply_operator(field, extend(field), modulus, padded_modulus)

    solution = jnp.zeros_like(load)
    residual = load
    image = operate(residual)
    norm_now, product = two_products(residual, image)
    alpha = norm_now / product
    direction, along_image = (residual, image)
    for number in range(ITERS):
        solution = solution + alpha * direction
        residual = residual - alpha * along_image
        if number + 1 < ITERS:
            image = operate(residual)
            norm_next, product = two_products(residual, image)
            ratio = norm_next / norm_now
            alpha = norm_next / (product - ratio * norm_next / alpha)
            direction = residual + ratio * direction
            along_image = image + ratio * along_image
            norm_now = norm_next
    joined = lax.all_to_all(
        jnp.concatenate([solution, residual]), "gz", split_axis=1, concat_axis=3, tiled=True
    )
    solution = joined[:3]
    residual = joined[3:]
    return (warmed_result, solution, residual)


def solution(mesh):
    in_specs = (
        P(None, "gx", ("gy", "gz")),
        P(None, "gx", ("gy", "gz")),
        P(None, "gx", ("gy", "gz")),
        P(),
        P(),
    )
    out_specs = (P(None, "gx", ("gy", "gz")), P(None, "gz", "gx", "gy"), P(None, "gz", "gx", "gy"))
    return jax.shard_map(
        per_device, mesh=mesh, in_specs=in_specs, out_specs=out_specs, check_vma=False
    )
```

profile of v0, /device:TPU:0, one launch (start us, length us, event | category | flops | bytes accessed | tf_op | source)
XLA Modules:
  0.0 370.7 jit_solution(7479689364601131842)
XLA Ops:
  9.6 4.9 %collective-permute-start = (f32[2,16,1,128]{3,1,2,0:T(8,128)S(1)}, f32[2,16,1,128]{3,1,2,0:T(8,128)S(1)}, u32[]{:S(2)}, u32[]{:S(2)}) collective-permute-start(f32[2,16,1,128]{3,1,2,0:T(8,128)S(1)} %get-tuple-element.112), channel_id=1, source_target_pairs={{0,16},{1,17},{2,18},{3,19},{4,20},{5,21},{6,22},{7,23},{8,24},{9,... | collective-permute-start | bytes 49160 | tf_op jit(solution)/shard_map/ppermute | solution.py:19
  15.9 4.2 %collective-permute-done.1 = f32[2,16,1,128]{3,1,2,0:T(8,128)S(1)} collective-permute-done((f32[2,16,1,128]{3,1,2,0:T(8,128)S(1)}, f32[2,16,1,128]{3,1,2,0:T(8,128)S(1)}, u32[]{:S(2)}, u32[]{:S(2)}) %collective-permute-start.1) | collective-permute-done | bytes 16416 | tf_op jit(solution)/shard_map/ppermute | solution.py:20
  25.8 8.3 %collective-permute-done.2 = f32[2,16,18,1]{3,1,2,0:T(8,128)S(1)} collective-permute-done((f32[2,16,18,1]{3,1,2,0:T(8,128)S(1)}, f32[2,16,18,1]{3,1,2,0:T(8,128)S(1)}, u32[]{:S(2)}, u32[]{:S(2)}) %collective-permute-start.2) | collective-permute-done | bytes 2336 | tf_op jit(solution)/shard_map/ppermute | solution.py:19
  35.3 13.0 %fusion.8 = f32[16,16,128]{2,0,1:T(8,128)S(1)} fusion(f32[16,16,128]{2,0,1:T(8,128)S(1)} %slice.2049, f32[16,18,130]{2,0,1:T(8,128)S(1)} %get-tuple-element.91, pred[16,16,128]{2,0,1:T(8,128)(4,1)S(1)} %get-tuple-element.74, f32[]{:T(128)} %bitcast.10, pred[16,16,128]{2,0,1:T(8,128)(4,1)S(1)} %get-tuple-element.73, f32[]{:T(128)} %bitcast.9, ...), kind=kLoop, calls=%fused_computation.73 | loop fusion | flops 3342336 | bytes 1835088 | tf_op jit(solution)/shard_map/add | solution.py:55
  55.6 4.8 %collective-permute-start.6 = (f32[16,18,1]{2,0,1:T(8,128)S(1)}, f32[16,18,1]{2,0,1:T(8,128)S(1)}, u32[]{:S(2)}, u32[]{:S(2)}) collective-permute-start(f32[16,18,1]{2,0,1:T(8,128)S(1)} %get-tuple-element.114), channel_id=1, source_target_pairs={{0,1},{1,2},{2,3},{3,4},{4,5},{5,6},{6,7},{7,8},{8,9},{9,10},{10,1... | collective-permute-start | bytes 3464 | tf_op jit(solution)/shard_map/ppermute | solution.py:19
  63.3 5.1 %collective-permute-done.7 = f32[16,18,1]{2,0,1:T(8,128)S(1)} collective-permute-done((f32[16,18,1]{2,0,1:T(8,128)S(1)}, f32[16,18,1]{2,0,1:T(8,128)S(1)}, u32[]{:S(2)}, u32[]{:S(2)}) %collective-permute-start.7) | collective-permute-done | bytes 1184 | tf_op jit(solution)/shard_map/ppermute | solution.py:20
  68.3 15.6 %add_multiply_fusion.6 = (f32[16,16,128]{2,0,1:T(8,128)S(1)}, f32[16,16,128]{2,0,1:T(8,128)S(1)}) fusion(pred[16,16,128]{2,0,1:T(8,128)(4,1)S(1)} %get-tuple-element.74, pred[16,16,128]{2,0,1:T(8,128)(4,1)S(1)} %get-tuple-element.73, pred[16,16,128]{2,0,1:T(8,128)(4,1)S(1)} %get-tuple-element.72, pred[16,16,128]{2,0,1:T(8,128)(4,1)S(1)} %get-tuple-element.71, ...), kind=kLoop, calls=%fused_computation.625 | loop fusion | flops 3866624 | bytes 1460576 | tf_op jit(solution)/shard_map/mul | solution.py:130
  94.1 5.2 %collective-permute-done.10 = f32[2,16,18,1]{3,1,2,0:T(8,128)S(1)} collective-permute-done((f32[2,16,18,1]{3,1,2,0:T(8,128)S(1)}, f32[2,16,18,1]{3,1,2,0:T(8,128)S(1)}, u32[]{:S(2)}, u32[]{:S(2)}) %collective-permute-start.10) | collective-permute-done | bytes 2336 | tf_op jit(solution)/shard_map/ppermute | solution.py:19
  99.3 4.7 %collective-permute-done.11 = f32[2,16,18,1]{3,1,2,0:T(8,128)S(1)} collective-permute-done((f32[2,16,18,1]{3,1,2,0:T(8,128)S(1)}, f32[2,16,18,1]{3,1,2,0:T(8,128)S(1)}, u32[]{:S(2)}, u32[]{:S(2)}) %collective-permute-start.11) | collective-permute-done | bytes 2336 | tf_op jit(solution)/shard_map/ppermute | solution.py:20
  118.4 4.2 %collective-permute-done.13 = f32[3,16,1,128]{3,1,2,0:T(8,128)S(1)} collective-permute-done((f32[3,16,1,128]{3,1,2,0:T(8,128)S(1)}, f32[3,16,1,128]{3,1,2,0:T(8,128)S(1)}, u32[]{:S(2)}, u32[]{:S(2)}) %collective-permute-start.13) | collective-permute-done | bytes 24608 | tf_op jit(solution)/shard_map/ppermute | solution.py:20
  123.3 6.3 %collective-permute-start.14 = (f32[3,16,18,1]{2,1,3,0:T(8,128)S(1)}, f32[3,16,18,1]{2,1,3,0:T(8,128)S(1)}, u32[]{:S(2)}, u32[]{:S(2)}) collective-permute-start(f32[3,16,18,1]{2,1,3,0:T(8,128)S(1)} %copy.174), channel_id=1, source_target_pairs={{0,1},{1,2},{2,3},{3,4},{4,5},{5,6},{6,7},{7,8},{8,9},{9,10},{10,1... | collective-permute-start | bytes 10376 | tf_op jit(solution)/shard_map/ppermute | solution.py:19
  137.0 5.2 %add_bitcast_fusion.7 = f32[1,16,16,128]{3,1,2,0:T(8,128)S(1)} fusion(f32[16,16,128]{2,0,1:T(8,128)S(1)} %fusion.52, f32[16,16,128]{2,0,1:T(8,128)S(1)} %fusion.93, f32[18,18,130]{2,0,1:T(8,128)S(1)} %get-tuple-element.85, f32[18,18,130]{2,0,1:T(8,128)S(1)} %get-tuple-element.84, f32[16,16,128]{2,0,1:T(8,128)S(1)} %fusion.31, ...), kind=kLoop, calls=%fused_computation.599 | loop fusion | flops 11862016 | bytes 14286864 | tf_op jit(solution)/shard_map/stack | solution.py:89
  142.2 5.2 %add_bitcast_fusion.6 = f32[1,16,16,128]{3,1,2,0:T(8,128)S(1)} fusion(f32[16,16,128]{2,0,1:T(8,128)S(1)} %fusion.31, f32[16,16,128]{2,0,1:T(8,128)S(1)} %fusion.93, f32[18,18,130]{2,0,1:T(8,128)S(1)} %get-tuple-element.85, f32[16,16,128]{2,0,1:T(8,128)S(1)} %fusion.52, f32[18,18,130]{2,0,1:T(8,128)S(1)} %get-tuple-element.84, ...), kind=kLoop, calls=%fused_computation.598 | loop fusion | flops 11862016 | bytes 14286864 | tf_op jit(solution)/shard_map/stack | solution.py:89
  147.4 5.2 %add_bitcast_fusion.8 = f32[1,16,16,128]{3,1,2,0:T(8,128)S(1)} fusion(f32[16,16,128]{2,0,1:T(8,128)S(1)} %fusion.93, f32[18,18,130]{2,0,1:T(8,128)S(1)} %get-tuple-element.85, f32[16,16,128]{2,0,1:T(8,128)S(1)} %fusion.52, f32[18,18,130]{2,0,1:T(8,128)S(1)} %get-tuple-element.84, f32[16,16,128]{2,0,1:T(8,128)S(1)} %fusion.31, ...), kind=kLoop, calls=%fused_computation.600 | loop fusion | flops 11862016 | bytes 14286864 | tf_op jit(solution)/shard_map/stack | solution.py:89
  153.3 40.6 %all-reduce.9 = (f32[]{:T(128)}, f32[]{:T(128)}) all-reduce(f32[]{:T(128)} %get-tuple-element.17, f32[]{:T(128)} %get-tuple-element.16), channel_id=1, replica_groups=mesh['gx'=2,'gy'=8,'gz'=2] {'gx','gy','gz'}, use_global_device_ids=true, to_apply=%region_1.2 | all-reduce | flops 2 | bytes 16 | tf_op jit(solution)/shard_map/psum | solution.py:111
  195.3 4.4 %collective-permute-start.16 = (f32[3,16,1,128]{3,1,2,0:T(8,128)S(1)}, f32[3,16,1,128]{3,1,2,0:T(8,128)S(1)}, u32[]{:S(2)}, u32[]{:S(2)}) collective-permute-start(f32[3,16,1,128]{3,1,2,0:T(8,128)S(1)} %get-tuple-element.102), channel_id=1, source_target_pairs={{0,16},{1,17},{2,18},{3,19},{4,20},{5,21},{6,22},{7,23},{8,24},{9,... | collective-permute-start | bytes 73736 | tf_op jit(solution)/shard_map/ppermute | solution.py:19
  201.2 4.2 %collective-permute-done.17 = f32[3,16,1,128]{3,1,2,0:T(8,128)S(1)} collective-permute-done((f32[3,16,1,128]{3,1,2,0:T(8,128)S(1)}, f32[3,16,1,128]{3,1,2,0:T(8,128)S(1)}, u32[]{:S(2)}, u32[]{:S(2)}) %collective-permute-start.17) | collective-permute-done | bytes 24608 | tf_op jit(solution)/shard_map/ppermute | solution.py:20
  215.3 5.4 %add_bitcast_fusion.5 = (f32[1,16,16,128]{3,1,2,0:T(8,128)S(1)}, f32[16,16,128]{2,0,1:T(8,128)S(1)}, f32[16,16,128]{2,0,1:T(8,128)S(1)}, f32[16,16,128]{2,0,1:T(...) fusion(f32[18,18,130]{2,0,1:T(8,128)S(1)} %get-tuple-element.82, ...), kind=kLoop, calls=%fused_computation.573 | loop fusion | flops 11862016 | bytes 17170448 | tf_op jit(solution)/shard_map/stack | solution.py:89
  229.7 39.7 %all-reduce.8 = (f32[]{:T(128)}, f32[]{:T(128)}) all-reduce(f32[]{:T(128)} %get-tuple-element.15, f32[]{:T(128)} %get-tuple-element.14), channel_id=1, replica_groups=mesh['gx'=2,'gy'=8,'gz'=2] {'gx','gy','gz'}, use_global_device_ids=true, to_apply=%region_5.6 | all-reduce | flops 2 | bytes 16 | tf_op jit(solution)/shard_map/psum | solution.py:111
  274.2 4.4 %collective-permute-start.20 = (f32[3,16,1,128]{3,1,2,0:T(8,128)S(1)}, f32[3,16,1,128]{3,1,2,0:T(8,128)S(1)}, u32[]{:S(2)}, u32[]{:S(2)}) collective-permute-start(f32[3,16,1,128]{3,1,2,0:T(8,128)S(1)} %get-tuple-element.100), channel_id=1, source_target_pairs={{0,16},{1,17},{2,18},{3,19},{4,20},{5,21},{6,22},{7,23},{8,24},{9,... | collective-permute-start | bytes 73736 | tf_op jit(solution)/shard_map/ppermute | solution.py:19
  280.1 4.2 %collective-permute-done.21 = f32[3,16,1,128]{3,1,2,0:T(8,128)S(1)} collective-permute-done((f32[3,16,1,128]{3,1,2,0:T(8,128)S(1)}, f32[3,16,1,128]{3,1,2,0:T(8,128)S(1)}, u32[]{:S(2)}, u32[]{:S(2)}) %collective-permute-start.21) | collective-permute-done | bytes 24608 | tf_op jit(solution)/shard_map/ppermute | solution.py:20
  294.1 5.4 %add_bitcast_fusion.2 = (f32[1,16,16,128]{3,1,2,0:T(8,128)S(1)}, f32[16,16,128]{2,0,1:T(8,128)S(1)}, f32[16,16,128]{2,0,1:T(8,128)S(1)}, f32[16,16,128]{2,0,1:T(...) fusion(f32[18,18,130]{2,0,1:T(8,128)S(1)} %get-tuple-element.79, ...), kind=kLoop, calls=%fused_computation.546 | loop fusion | flops 11862016 | bytes 17170448 | tf_op jit(solution)/shard_map/stack | solution.py:89
  308.6 39.8 %all-reduce.7 = (f32[]{:T(128)}, f32[]{:T(128)}) all-reduce(f32[]{:T(128)} %get-tuple-element.13, f32[]{:T(128)} %get-tuple-element.12), channel_id=1, replica_groups=mesh['gx'=2,'gy'=8,'gz'=2] {'gx','gy','gz'}, use_global_device_ids=true, to_apply=%region_9.10 | all-reduce | flops 2 | bytes 16 | tf_op jit(solution)/shard_map/psum | solution.py:111
  358.2 9.7 %all-to-all-done = f32[6,16,16,128]{3,2,0,1:T(8,128)S(1)} async-done(((f32[6,16,16,128]{3,2,0,1:T(8,128)}), f32[6,16,16,128]{3,2,0,1:T(8,128)S(1)}, u32[]{:S(2)}, u32[]{:S(2)}) %all-to-all-start) | async-done | bytes 786464 | tf_op jit(solution)/shard_map/all_to_all | solution.py:162
  (108 shorter events, 109.9 us)
Async XLA Ops:
  9.6 6.3 %collective-permute-start = (f32[2,16,1,128]{3,1,2,0:T(8,128)S(1)}, f32[2,16,1,128]{3,1,2,0:T(8,128)S(1)}, u32[]{:S(2)}, u32[]{:S(2)}) collective-permute-start(f32[2,16,1,128]{3,1,2,0:T(8,128)S(1)} %get-tuple-element.112), channel_id=1, source_target_pairs={{0,16},{1,17},{2,18},{3,19},{4,20},{5,21},{6,22},{7,23},{8,24},{9,... | collective-permute-start | bytes 49160 | tf_op jit(solution)/shard_map/ppermute | solution.py:19
  14.5 5.6 %collective-permute-start.1 = (f32[2,16,1,128]{3,1,2,0:T(8,128)S(1)}, f32[2,16,1,128]{3,1,2,0:T(8,128)S(1)}, u32[]{:S(2)}, u32[]{:S(2)}) collective-permute-start(f32[2,16,1,128]{3,1,2,0:T(8,128)S(1)} %get-tuple-element.113), channel_id=1, source_target_pairs={{16,0},{17,1},{18,2},{19,3},{20,4},{21,5},{22,6},{23,7},{24,8},{25... | collective-permute-start | bytes 49160 | tf_op jit(solution)/shard_map/ppermute | solution.py:20
  20.3 13.8 %collective-permute-start.2 = (f32[2,16,18,1]{3,1,2,0:T(8,128)S(1)}, f32[2,16,18,1]{3,1,2,0:T(8,128)S(1)}, u32[]{:S(2)}, u32[]{:S(2)}) collective-permute-start(f32[2,16,18,1]{3,1,2,0:T(8,128)S(1)} %get-tuple-element.108), channel_id=1, source_target_pairs={{0,1},{1,2},{2,3},{3,4},{4,5},{5,6},{6,7},{7,8},{8,9},{9,10},{10,1... | collective-permute-start | bytes 6920 | tf_op jit(solution)/shard_map/ppermute | solution.py:19
  23.7 11.0 %collective-permute-start.3 = (f32[2,16,18,1]{3,1,2,0:T(8,128)S(1)}, f32[2,16,18,1]{3,1,2,0:T(8,128)S(1)}, u32[]{:S(2)}, u32[]{:S(2)}) collective-permute-start(f32[2,16,18,1]{3,1,2,0:T(8,128)S(1)} %get-tuple-element.109), channel_id=1, source_target_pairs={{1,0},{2,1},{3,2},{4,3},{5,4},{6,5},{7,6},{8,7},{9,8},{10,9},{11,1... | collective-permute-start | bytes 6920 | tf_op jit(solution)/shard_map/ppermute | solution.py:20
  49.9 5.5 %collective-permute-start.5 = (f32[16,1,128]{2,0,1:T(8,128)S(1)}, f32[16,1,128]{2,0,1:T(8,128)S(1)}, u32[]{:S(2)}, u32[]{:S(2)}) collective-permute-start(f32[16,1,128]{2,0,1:T(8,128)S(1)} %get-tuple-element.117), channel_id=1, source_target_pairs={{16,0},{17,1},{18,2},{19,3},{20,4},{21,5},{22,6},{23,7},{24,8},{25... | collective-permute-start | bytes 24584 | tf_op jit(solution)/shard_map/ppermute | solution.py:20
  55.6 7.7 %collective-permute-start.6 = (f32[16,18,1]{2,0,1:T(8,128)S(1)}, f32[16,18,1]{2,0,1:T(8,128)S(1)}, u32[]{:S(2)}, u32[]{:S(2)}) collective-permute-start(f32[16,18,1]{2,0,1:T(8,128)S(1)} %get-tuple-element.114), channel_id=1, source_target_pairs={{0,1},{1,2},{2,3},{3,4},{4,5},{5,6},{6,7},{7,8},{8,9},{9,10},{10,1... | collective-permute-start | bytes 3464 | tf_op jit(solution)/shard_map/ppermute | solution.py:19
  60.4 7.9 %collective-permute-start.7 = (f32[16,18,1]{2,0,1:T(8,128)S(1)}, f32[16,18,1]{2,0,1:T(8,128)S(1)}, u32[]{:S(2)}, u32[]{:S(2)}) collective-permute-start(f32[16,18,1]{2,0,1:T(8,128)S(1)} %get-tuple-element.115), channel_id=1, source_target_pairs={{1,0},{2,1},{3,2},{4,3},{5,4},{6,5},{7,6},{8,7},{9,8},{10,9},{11,1... | collective-permute-start | bytes 3464 | tf_op jit(solution)/shard_map/ppermute | solution.py:20
  83.9 3.1 collective-permute-start.8
  85.5 5.6 %collective-permute-start.9 = (f32[2,16,1,128]{3,1,2,0:T(8,128)S(1)}, f32[2,16,1,128]{3,1,2,0:T(8,128)S(1)}, u32[]{:S(2)}, u32[]{:S(2)}) collective-permute-start(f32[2,16,1,128]{3,1,2,0:T(8,128)S(1)} %get-tuple-element.111), channel_id=1, source_target_pairs={{16,0},{17,1},{18,2},{19,3},{20,4},{21,5},{22,6},{23,7},{24,8},{25... | collective-permute-start | bytes 49160 | tf_op jit(solution)/shard_map/ppermute | solution.py:20
  91.4 7.9 %collective-permute-start.10 = (f32[2,16,18,1]{3,1,2,0:T(8,128)S(1)}, f32[2,16,18,1]{3,1,2,0:T(8,128)S(1)}, u32[]{:S(2)}, u32[]{:S(2)}) collective-permute-start(f32[2,16,18,1]{3,1,2,0:T(8,128)S(1)} %get-tuple-element.106), channel_id=1, source_target_pairs={{0,1},{1,2},{2,3},{3,4},{4,5},{5,6},{6,7},{7,8},{8,9},{9,10},{10,1... | collective-permute-start | bytes 6920 | tf_op jit(solution)/shard_map/ppermute | solution.py:19
  92.8 11.1 %collective-permute-start.11 = (f32[2,16,18,1]{3,1,2,0:T(8,128)S(1)}, f32[2,16,18,1]{3,1,2,0:T(8,128)S(1)}, u32[]{:S(2)}, u32[]{:S(2)}) collective-permute-start(f32[2,16,18,1]{3,1,2,0:T(8,128)S(1)} %get-tuple-element.107), channel_id=1, source_target_pairs={{1,0},{2,1},{3,2},{4,3},{5,4},{6,5},{7,6},{8,7},{9,8},{10,9},{11,1... | collective-permute-start | bytes 6920 | tf_op jit(solution)/shard_map/ppermute | solution.py:20
  114.7 3.7 %collective-permute-start.12 = (f32[3,16,1,128]{3,1,2,0:T(8,128)S(1)}, f32[3,16,1,128]{3,1,2,0:T(8,128)S(1)}, u32[]{:S(2)}, u32[]{:S(2)}) collective-permute-start(f32[3,16,1,128]{3,1,2,0:T(8,128)S(1)} %get-tuple-element.104), channel_id=1, source_target_pairs={{0,16},{1,17},{2,18},{3,19},{4,20},{5,21},{6,22},{7,23},{8,24},{9,... | collective-permute-start | bytes 73736 | tf_op jit(solution)/shard_map/ppermute | solution.py:19
  116.9 5.7 %collective-permute-start.13 = (f32[3,16,1,128]{3,1,2,0:T(8,128)S(1)}, f32[3,16,1,128]{3,1,2,0:T(8,128)S(1)}, u32[]{:S(2)}, u32[]{:S(2)}) collective-permute-start(f32[3,16,1,128]{3,1,2,0:T(8,128)S(1)} %get-tuple-element.105), channel_id=1, source_target_pairs={{16,0},{17,1},{18,2},{19,3},{20,4},{21,5},{22,6},{23,7},{24,8},{25... | collective-permute-start | bytes 73736 | tf_op jit(solution)/shard_map/ppermute | solution.py:20
  123.3 8.2 %collective-permute-start.14 = (f32[3,16,18,1]{2,1,3,0:T(8,128)S(1)}, f32[3,16,18,1]{2,1,3,0:T(8,128)S(1)}, u32[]{:S(2)}, u32[]{:S(2)}) collective-permute-start(f32[3,16,18,1]{2,1,3,0:T(8,128)S(1)} %copy.174), channel_id=1, source_target_pairs={{0,1},{1,2},{2,3},{3,4},{4,5},{5,6},{6,7},{7,8},{8,9},{9,10},{10,1... | collective-permute-start | bytes 10376 | tf_op jit(solution)/shard_map/ppermute | solution.py:19
  130.0 5.8 %collective-permute-start.15 = (f32[3,16,18,1]{2,1,3,0:T(8,128)S(1)}, f32[3,16,18,1]{2,1,3,0:T(8,128)S(1)}, u32[]{:S(2)}, u32[]{:S(2)}) collective-permute-start(f32[3,16,18,1]{2,1,3,0:T(8,128)S(1)} %copy.175), channel_id=1, source_target_pairs={{1,0},{2,1},{3,2},{4,3},{5,4},{6,5},{7,6},{8,7},{9,8},{10,9},{11,1... | collective-permute-start | bytes 10376 | tf_op jit(solution)/shard_map/ppermute | solution.py:20
  195.3 5.9 %collective-permute-start.16 = (f32[3,16,1,128]{3,1,2,0:T(8,128)S(1)}, f32[3,16,1,128]{3,1,2,0:T(8,128)S(1)}, u32[]{:S(2)}, u32[]{:S(2)}) collective-permute-start(f32[3,16,1,128]{3,1,2,0:T(8,128)S(1)} %get-tuple-element.102), channel_id=1, source_target_pairs={{0,16},{1,17},{2,18},{3,19},{4,20},{5,21},{6,22},{7,23},{8,24},{9,... | collective-permute-start | bytes 73736 | tf_op jit(solution)/shard_map/ppermute | solution.py:19
  199.7 5.7 %collective-permute-start.17 = (f32[3,16,1,128]{3,1,2,0:T(8,128)S(1)}, f32[3,16,1,128]{3,1,2,0:T(8,128)S(1)}, u32[]{:S(2)}, u32[]{:S(2)}) collective-permute-start(f32[3,16,1,128]{3,1,2,0:T(8,128)S(1)} %get-tuple-element.103), channel_id=1, source_target_pairs={{16,0},{17,1},{18,2},{19,3},{20,4},{21,5},{22,6},{23,7},{24,8},{25... | collective-permute-start | bytes 73736 | tf_op jit(solution)/shard_map/ppermute | solution.py:20
  206.0 3.9 %collective-permute-start.18 = (f32[3,16,18,1]{2,1,3,0:T(8,128)S(1)}, f32[3,16,18,1]{2,1,3,0:T(8,128)S(1)}, u32[]{:S(2)}, u32[]{:S(2)}) collective-permute-start(f32[3,16,18,1]{2,1,3,0:T(8,128)S(1)} %copy.190), channel_id=1, source_target_pairs={{0,1},{1,2},{2,3},{3,4},{4,5},{5,6},{6,7},{7,8},{8,9},{9,10},{10,1... | collective-permute-start | bytes 10376 | tf_op jit(solution)/shard_map/ppermute | solution.py:19
  208.5 5.7 %collective-permute-start.19 = (f32[3,16,18,1]{2,1,3,0:T(8,128)S(1)}, f32[3,16,18,1]{2,1,3,0:T(8,128)S(1)}, u32[]{:S(2)}, u32[]{:S(2)}) collective-permute-start(f32[3,16,18,1]{2,1,3,0:T(8,128)S(1)} %copy.191), channel_id=1, source_target_pairs={{1,0},{2,1},{3,2},{4,3},{5,4},{6,5},{7,6},{8,7},{9,8},{10,9},{11,1... | collective-permute-start | bytes 10376 | tf_op jit(solution)/shard_map/ppermute | solution.py:20
  274.2 5.9 %collective-permute-start.20 = (f32[3,16,1,128]{3,1,2,0:T(8,128)S(1)}, f32[3,16,1,128]{3,1,2,0:T(8,128)S(1)}, u32[]{:S(2)}, u32[]{:S(2)}) collective-permute-start(f32[3,16,1,128]{3,1,2,0:T(8,128)S(1)} %get-tuple-element.100), channel_id=1, source_target_pairs={{0,16},{1,17},{2,18},{3,19},{4,20},{5,21},{6,22},{7,23},{8,24},{9,... | collective-permute-start | bytes 73736 | tf_op jit(solution)/shard_map/ppermute | solution.py:19
  278.6 5.7 %collective-permute-start.21 = (f32[3,16,1,128]{3,1,2,0:T(8,128)S(1)}, f32[3,16,1,128]{3,1,2,0:T(8,128)S(1)}, u32[]{:S(2)}, u32[]{:S(2)}) collective-permute-start(f32[3,16,1,128]{3,1,2,0:T(8,128)S(1)} %get-tuple-element.101), channel_id=1, source_target_pairs={{16,0},{17,1},{18,2},{19,3},{20,4},{21,5},{22,6},{23,7},{24,8},{25... | collective-permute-start | bytes 73736 | tf_op jit(solution)/shard_map/ppermute | solution.py:20
  285.0 3.9 %collective-permute-start.22 = (f32[3,16,18,1]{2,1,3,0:T(8,128)S(1)}, f32[3,16,18,1]{2,1,3,0:T(8,128)S(1)}, u32[]{:S(2)}, u32[]{:S(2)}) collective-permute-start(f32[3,16,18,1]{2,1,3,0:T(8,128)S(1)} %copy.192), channel_id=1, source_target_pairs={{0,1},{1,2},{2,3},{3,4},{4,5},{5,6},{6,7},{7,8},{8,9},{9,10},{10,1... | collective-permute-start | bytes 10376 | tf_op jit(solution)/shard_map/ppermute | solution.py:19
  287.3 5.7 %collective-permute-start.23 = (f32[3,16,18,1]{2,1,3,0:T(8,128)S(1)}, f32[3,16,18,1]{2,1,3,0:T(8,128)S(1)}, u32[]{:S(2)}, u32[]{:S(2)}) collective-permute-start(f32[3,16,18,1]{2,1,3,0:T(8,128)S(1)} %copy.193), channel_id=1, source_target_pairs={{1,0},{2,1},{3,2},{4,3},{5,4},{6,5},{7,6},{8,7},{9,8},{10,9},{11,1... | collective-permute-start | bytes 10376 | tf_op jit(solution)/shard_map/ppermute | solution.py:20
  353.9 14.0 %all-to-all-start = ((f32[6,16,16,128]{3,2,0,1:T(8,128)}), f32[6,16,16,128]{3,2,0,1:T(8,128)S(1)}, u32[]{:S(2)}, u32[]{:S(2)}) async-start(f32[6,16,16,128]{3,2,0,1:T(8,128)} %copy.186), calls=%async_computation | async-start | bytes 1572864 | tf_op jit(solution)/shard_map/all_to_all | solution.py:162
  (3 other events, 31.5 us)
where the time goes:
time: 373 us; the launch traced here: 371 us
  blocking collectives  120 us (32%)
  other arithmetic  94.1 us (25%)
  waiting for transfers between devices  72.8 us (20%)
  starting transfers between devices  58.9 us (16%)
  local copies, waits for them, and re-layouts  13.6 us (4%)
  between operations  11.3 us (3%)
    psum x3, blocking collectives, two_products(): lax.psum((jnp.sum(residual * residual), jnp.sum(residual * image)), ('gx'...  120 us
    ppermute x12, waiting for transfers between devices, padded(): after = lax.ppermute(initial, axis, down)  47.1 us
    another operation x9, other arithmetic, apply_operator(): return jnp.stack(parts)  42.9 us
    ppermute x12, starting transfers between devices, padded(): before = lax.ppermute(last, axis, up)  39.2 us
    ppermute x12, starting transfers between devices, padded(): after = lax.ppermute(initial, axis, down)  16.1 us
    ppermute x12, waiting for transfers between devices, padded(): before = lax.ppermute(last, axis, up)  16 us
    mul x1, other arithmetic, per_device(): strain = lookup(substance_label, substance_traits[3], count) * warmed_result  15.6 us
    add x1, other arithmetic, heat_step(): return centre + time_step * inverse_cap * (heat_flux + power)  13 us
  transfers between devices with their start and end apart: 25, of which 21 were waited for; matrix products, arithmetic and copies ran while one was open for 1% of the time, Pallas kernels for 0%

commit v1 on v0

--- a/solution.py
+++ b/solution.py
@@ -108,7 +108,9 @@
 
 
 def two_products(residual, image):
-    return lax.psum((jnp.sum(residual * residual), jnp.sum(residual * image)), ("gx", "gy", "gz"))
+    return lax.psum(
+        lax.psum((jnp.sum(residual * residual), jnp.sum(residual * image)), ("gy", "gz")), "gx"
+    )
 
 
 def per_device(

time: 373 us -> 359 us (0.962)
  blocking collectives: 120 us -> 107 us
    psum x3 -> x6, blocking collectives: 120 us -> 107 us  [the longest x3 90.8 us: two_products(): lax.psum((jnp.sum(residual * residual), jnp.sum(residual * image)), ('gy'...]
where the time goes in v1:
time: 359 us; the launch traced here: 357 us
  blocking collectives  107 us (30%)
  other arithmetic  96 us (27%)
  waiting for transfers between devices  70.7 us (20%)
  starting transfers between devices  57.9 us (16%)
  local copies, waits for them, and re-layouts  13.6 us (4%)
  between operations  11.3 us (3%)
    psum x3, blocking collectives, two_products(): lax.psum((jnp.sum(residual * residual), jnp.sum(residual * image)), ('gy'...  90.8 us
    ppermute x12, waiting for transfers between devices, padded(): after = lax.ppermute(initial, axis, down)  47.1 us
    another operation x9, other arithmetic, apply_operator(): return jnp.stack(parts)  44.1 us
    ppermute x12, starting transfers between devices, padded(): before = lax.ppermute(last, axis, up)  38.2 us
    psum x3, blocking collectives, two_products(): lax.psum(lax.psum((jnp.sum(residual * residual), jnp.sum(residual * image...  16.7 us
    ppermute x12, starting transfers between devices, padded(): after = lax.ppermute(initial, axis, down)  16.1 us
    ppermute x12, waiting for transfers between devices, padded(): before = lax.ppermute(last, axis, up)  16 us
    mul x1, other arithmetic, per_device(): strain = lookup(substance_label, substance_traits[3], count) * warmed_result  15.6 us
  transfers between devices with their start and end apart: 25, of which 21 were waited for; matrix products, arithmetic and copies ran while one was open for 1% of the time, Pallas kernels for 0%

profile of v1, /device:TPU:0, one launch (start us, length us, event | category | flops | bytes accessed | tf_op | source)
XLA Modules:
  0.0 357.0 jit_solution(14091216128686443268)
XLA Ops:
  9.8 4.9 %collective-permute-start = (f32[2,16,1,128]{3,1,2,0:T(8,128)S(1)}, f32[2,16,1,128]{3,1,2,0:T(8,128)S(1)}, u32[]{:S(2)}, u32[]{:S(2)}) collective-permute-start(f32[2,16,1,128]{3,1,2,0:T(8,128)S(1)} %get-tuple-element.118), channel_id=1, source_target_pairs={{0,16},{1,17},{2,18},{3,19},{4,20},{5,21},{6,22},{7,23},{8,24},{9,... | collective-permute-start | bytes 49160 | tf_op jit(solution)/shard_map/ppermute | solution.py:19
  26.0 8.3 %collective-permute-done.2 = f32[2,16,18,1]{3,1,2,0:T(8,128)S(1)} collective-permute-done((f32[2,16,18,1]{3,1,2,0:T(8,128)S(1)}, f32[2,16,18,1]{3,1,2,0:T(8,128)S(1)}, u32[]{:S(2)}, u32[]{:S(2)}) %collective-permute-start.2) | collective-permute-done | bytes 2336 | tf_op jit(solution)/shard_map/ppermute | solution.py:19
  35.5 13.0 %fusion.8 = f32[16,16,128]{2,0,1:T(8,128)S(1)} fusion(f32[16,16,128]{2,0,1:T(8,128)S(1)} %slice.2049, f32[16,18,130]{2,0,1:T(8,128)S(1)} %get-tuple-element.97, pred[16,16,128]{2,0,1:T(8,128)(4,1)S(1)} %get-tuple-element.80, f32[]{:T(128)} %bitcast.10, pred[16,16,128]{2,0,1:T(8,128)(4,1)S(1)} %get-tuple-element.79, f32[]{:T(128)} %bitcast.9, ...), kind=kLoop, calls=%fused_computation.73 | loop fusion | flops 3342336 | bytes 1835088 | tf_op jit(solution)/shard_map/add | solution.py:55
  55.8 4.8 %collective-permute-start.6 = (f32[16,18,1]{2,0,1:T(8,128)S(1)}, f32[16,18,1]{2,0,1:T(8,128)S(1)}, u32[]{:S(2)}, u32[]{:S(2)}) collective-permute-start(f32[16,18,1]{2,0,1:T(8,128)S(1)} %get-tuple-element.120), channel_id=1, source_target_pairs={{0,1},{1,2},{2,3},{3,4},{4,5},{5,6},{6,7},{7,8},{8,9},{9,10},{10,1... | collective-permute-start | bytes 3464 | tf_op jit(solution)/shard_map/ppermute | solution.py:19
  63.5 5.1 %collective-permute-done.7 = f32[16,18,1]{2,0,1:T(8,128)S(1)} collective-permute-done((f32[16,18,1]{2,0,1:T(8,128)S(1)}, f32[16,18,1]{2,0,1:T(8,128)S(1)}, u32[]{:S(2)}, u32[]{:S(2)}) %collective-permute-start.7) | collective-permute-done | bytes 1184 | tf_op jit(solution)/shard_map/ppermute | solution.py:20
  68.6 15.6 %add_multiply_fusion.6 = (f32[16,16,128]{2,0,1:T(8,128)S(1)}, f32[16,16,128]{2,0,1:T(8,128)S(1)}) fusion(pred[16,16,128]{2,0,1:T(8,128)(4,1)S(1)} %get-tuple-element.80, pred[16,16,128]{2,0,1:T(8,128)(4,1)S(1)} %get-tuple-element.79, pred[16,16,128]{2,0,1:T(8,128)(4,1)S(1)} %get-tuple-element.78, pred[16,16,128]{2,0,1:T(8,128)(4,1)S(1)} %get-tuple-element.77, ...), kind=kLoop, calls=%fused_computation.625 | loop fusion | flops 3866624 | bytes 1460576 | tf_op jit(solution)/shard_map/mul | solution.py:132
  94.4 5.2 %collective-permute-done.10 = f32[2,16,18,1]{3,1,2,0:T(8,128)S(1)} collective-permute-done((f32[2,16,18,1]{3,1,2,0:T(8,128)S(1)}, f32[2,16,18,1]{3,1,2,0:T(8,128)S(1)}, u32[]{:S(2)}, u32[]{:S(2)}) %collective-permute-start.10) | collective-permute-done | bytes 2336 | tf_op jit(solution)/shard_map/ppermute | solution.py:19
  99.5 4.7 %collective-permute-done.11 = f32[2,16,18,1]{3,1,2,0:T(8,128)S(1)} collective-permute-done((f32[2,16,18,1]{3,1,2,0:T(8,128)S(1)}, f32[2,16,18,1]{3,1,2,0:T(8,128)S(1)}, u32[]{:S(2)}, u32[]{:S(2)}) %collective-permute-start.11) | collective-permute-done | bytes 2336 | tf_op jit(solution)/shard_map/ppermute | solution.py:20
  123.9 6.3 %collective-permute-start.14 = (f32[3,16,18,1]{2,1,3,0:T(8,128)S(1)}, f32[3,16,18,1]{2,1,3,0:T(8,128)S(1)}, u32[]{:S(2)}, u32[]{:S(2)}) collective-permute-start(f32[3,16,18,1]{2,1,3,0:T(8,128)S(1)} %copy.174), channel_id=1, source_target_pairs={{0,1},{1,2},{2,3},{3,4},{4,5},{5,6},{6,7},{7,8},{8,9},{9,10},{10,1... | collective-permute-start | bytes 10376 | tf_op jit(solution)/shard_map/ppermute | solution.py:19
  137.6 5.3 %add_bitcast_fusion.7 = f32[1,16,16,128]{3,1,2,0:T(8,128)S(1)} fusion(f32[16,16,128]{2,0,1:T(8,128)S(1)} %fusion.52, f32[16,16,128]{2,0,1:T(8,128)S(1)} %fusion.93, f32[18,18,130]{2,0,1:T(8,128)S(1)} %get-tuple-element.91, f32[18,18,130]{2,0,1:T(8,128)S(1)} %get-tuple-element.90, f32[16,16,128]{2,0,1:T(8,128)S(1)} %fusion.31, ...), kind=kLoop, calls=%fused_computation.599 | loop fusion | flops 11862016 | bytes 14286864 | tf_op jit(solution)/shard_map/stack | solution.py:89
  143.0 5.3 %add_bitcast_fusion.6 = f32[1,16,16,128]{3,1,2,0:T(8,128)S(1)} fusion(f32[16,16,128]{2,0,1:T(8,128)S(1)} %fusion.31, f32[16,16,128]{2,0,1:T(8,128)S(1)} %fusion.93, f32[18,18,130]{2,0,1:T(8,128)S(1)} %get-tuple-element.91, f32[16,16,128]{2,0,1:T(8,128)S(1)} %fusion.52, f32[18,18,130]{2,0,1:T(8,128)S(1)} %get-tuple-element.90, ...), kind=kLoop, calls=%fused_computation.598 | loop fusion | flops 11862016 | bytes 14286864 | tf_op jit(solution)/shard_map/stack | solution.py:89
  148.3 5.3 %add_bitcast_fusion.8 = f32[1,16,16,128]{3,1,2,0:T(8,128)S(1)} fusion(f32[16,16,128]{2,0,1:T(8,128)S(1)} %fusion.93, f32[18,18,130]{2,0,1:T(8,128)S(1)} %get-tuple-element.91, f32[16,16,128]{2,0,1:T(8,128)S(1)} %fusion.52, f32[18,18,130]{2,0,1:T(8,128)S(1)} %get-tuple-element.90, f32[16,16,128]{2,0,1:T(8,128)S(1)} %fusion.31, ...), kind=kLoop, calls=%fused_computation.600 | loop fusion | flops 11862016 | bytes 14286864 | tf_op jit(solution)/shard_map/stack | solution.py:89
  154.4 30.5 %all-reduce.9 = (f32[]{:T(128)}, f32[]{:T(128)}) all-reduce(f32[]{:T(128)} %get-tuple-element.17, f32[]{:T(128)} %get-tuple-element.16), channel_id=1, replica_groups=mesh['gx'=2,'gy'=8,'gz'=2] {'gy','gz'}, use_global_device_ids=true, to_apply=%region_1.2 | all-reduce | flops 2 | bytes 16 | tf_op jit(solution)/shard_map/psum | solution.py:112
  184.9 5.5 %all-reduce.12 = (f32[]{:T(128)}, f32[]{:T(128)}) all-reduce(f32[]{:T(128)} %get-tuple-element.22, f32[]{:T(128)} %get-tuple-element.23), channel_id=1, replica_groups=mesh['gx'=2,'gy'=8,'gz'=2] {'gx'}, use_global_device_ids=true, to_apply=%region_2.3 | all-reduce | flops 2 | bytes 16 | tf_op jit(solution)/shard_map/psum | solution.py:111
  211.1 5.5 %add_bitcast_fusion.5 = (f32[1,16,16,128]{3,1,2,0:T(8,128)S(1)}, f32[16,16,128]{2,0,1:T(8,128)S(1)}, f32[16,16,128]{2,0,1:T(8,128)S(1)}, f32[16,16,128]{2,0,1:T(...) fusion(f32[18,18,130]{2,0,1:T(8,128)S(1)} %get-tuple-element.88, ...), kind=kLoop, calls=%fused_computation.573 | loop fusion | flops 11862016 | bytes 17170448 | tf_op jit(solution)/shard_map/stack | solution.py:89
  216.6 4.3 %add_bitcast_fusion.4 = f32[1,16,16,128]{3,1,2,0:T(8,128)S(1)} fusion(f32[16,16,128]{2,0,1:T(8,128)S(1)} %get-tuple-element.75, f32[16,16,128]{2,0,1:T(8,128)S(1)} %get-tuple-element.57, f32[16,16,128]{2,0,1:T(8,128)S(1)} %get-tuple-element.72, f32[16,16,128]{2,0,1:T(8,128)S(1)} %get-tuple-element.56, f32[16,16,128]{2,0,1:T(8,128)S(1)} %get-tuple-element.71, ...), kind=kLoop, calls=%fused_computation.572 | loop fusion | flops 7864320 | bytes 11403280 | tf_op jit(solution)/shard_map/stack | solution.py:89
  220.9 4.3 %add_bitcast_fusion.3 = f32[1,16,16,128]{3,1,2,0:T(8,128)S(1)} fusion(f32[16,16,128]{2,0,1:T(8,128)S(1)} %get-tuple-element.75, f32[16,16,128]{2,0,1:T(8,128)S(1)} %get-tuple-element.74, f32[16,16,128]{2,0,1:T(8,128)S(1)} %get-tuple-element.73, f32[16,16,128]{2,0,1:T(8,128)S(1)} %get-tuple-element.72, f32[16,16,128]{2,0,1:T(8,128)S(1)} %get-tuple-element.71, ...), kind=kLoop, calls=%fused_computation.571 | loop fusion | flops 7864320 | bytes 11403280 | tf_op jit(solution)/shard_map/stack | solution.py:89
  226.0 30.1 %all-reduce.8 = (f32[]{:T(128)}, f32[]{:T(128)}) all-reduce(f32[]{:T(128)} %get-tuple-element.15, f32[]{:T(128)} %get-tuple-element.14), channel_id=1, replica_groups=mesh['gx'=2,'gy'=8,'gz'=2] {'gy','gz'}, use_global_device_ids=true, to_apply=%region_7.8 | all-reduce | flops 2 | bytes 16 | tf_op jit(solution)/shard_map/psum | solution.py:112
  256.1 5.6 %all-reduce.11 = (f32[]{:T(128)}, f32[]{:T(128)}) all-reduce(f32[]{:T(128)} %get-tuple-element.20, f32[]{:T(128)} %get-tuple-element.21), channel_id=1, replica_groups=mesh['gx'=2,'gy'=8,'gz'=2] {'gx'}, use_global_device_ids=true, to_apply=%region_8.9 | all-reduce | flops 2 | bytes 16 | tf_op jit(solution)/shard_map/psum | solution.py:111
  286.2 5.5 %add_bitcast_fusion.2 = (f32[1,16,16,128]{3,1,2,0:T(8,128)S(1)}, f32[16,16,128]{2,0,1:T(8,128)S(1)}, f32[16,16,128]{2,0,1:T(8,128)S(1)}, f32[16,16,128]{2,0,1:T(...) fusion(f32[18,18,130]{2,0,1:T(8,128)S(1)} %get-tuple-element.85, ...), kind=kLoop, calls=%fused_computation.546 | loop fusion | flops 11862016 | bytes 17170448 | tf_op jit(solution)/shard_map/stack | solution.py:89
  291.7 4.3 %add_bitcast_fusion.1 = f32[1,16,16,128]{3,1,2,0:T(8,128)S(1)} fusion(f32[16,16,128]{2,0,1:T(8,128)S(1)} %get-tuple-element.52, f32[16,16,128]{2,0,1:T(8,128)S(1)} %get-tuple-element.34, f32[16,16,128]{2,0,1:T(8,128)S(1)} %get-tuple-element.49, f32[16,16,128]{2,0,1:T(8,128)S(1)} %get-tuple-element.33, f32[16,16,128]{2,0,1:T(8,128)S(1)} %get-tuple-element.48, ...), kind=kLoop, calls=%fused_computation.545 | loop fusion | flops 7864320 | bytes 11403280 | tf_op jit(solution)/shard_map/stack | solution.py:89
  301.1 30.1 %all-reduce.7 = (f32[]{:T(128)}, f32[]{:T(128)}) all-reduce(f32[]{:T(128)} %get-tuple-element.13, f32[]{:T(128)} %get-tuple-element.12), channel_id=1, replica_groups=mesh['gx'=2,'gy'=8,'gz'=2] {'gy','gz'}, use_global_device_ids=true, to_apply=%region_13.14 | all-reduce | flops 2 | bytes 16 | tf_op jit(solution)/shard_map/psum | solution.py:112
  331.2 5.5 %all-reduce.10 = (f32[]{:T(128)}, f32[]{:T(128)}) all-reduce(f32[]{:T(128)} %get-tuple-element.18, f32[]{:T(128)} %get-tuple-element.19), channel_id=1, replica_groups=mesh['gx'=2,'gy'=8,'gz'=2] {'gx'}, use_global_device_ids=true, to_apply=%region_14.15 | all-reduce | flops 2 | bytes 16 | tf_op jit(solution)/shard_map/psum | solution.py:111
  346.6 7.6 %all-to-all-done = f32[6,16,16,128]{3,2,0,1:T(8,128)S(1)} async-done(((f32[6,16,16,128]{3,2,0,1:T(8,128)}), f32[6,16,16,128]{3,2,0,1:T(8,128)S(1)}, u32[]{:S(2)}, u32[]{:S(2)}) %all-to-all-start) | async-done | bytes 786464 | tf_op jit(solution)/shard_map/all_to_all | solution.py:164
  (111 shorter events, 122.9 us)
Async XLA Ops:
  9.8 6.3 %collective-permute-start = (f32[2,16,1,128]{3,1,2,0:T(8,128)S(1)}, f32[2,16,1,128]{3,1,2,0:T(8,128)S(1)}, u32[]{:S(2)}, u32[]{:S(2)}) collective-permute-start(f32[2,16,1,128]{3,1,2,0:T(8,128)S(1)} %get-tuple-element.118), channel_id=1, source_target_pairs={{0,16},{1,17},{2,18},{3,19},{4,20},{5,21},{6,22},{7,23},{8,24},{9,... | collective-permute-start | bytes 49160 | tf_op jit(solution)/shard_map/ppermute | solution.py:19
  14.7 5.6 %collective-permute-start.1 = (f32[2,16,1,128]{3,1,2,0:T(8,128)S(1)}, f32[2,16,1,128]{3,1,2,0:T(8,128)S(1)}, u32[]{:S(2)}, u32[]{:S(2)}) collective-permute-start(f32[2,16,1,128]{3,1,2,0:T(8,128)S(1)} %get-tuple-element.119), channel_id=1, source_target_pairs={{16,0},{17,1},{18,2},{19,3},{20,4},{21,5},{22,6},{23,7},{24,8},{25... | collective-permute-start | bytes 49160 | tf_op jit(solution)/shard_map/ppermute | solution.py:20
  20.5 13.8 %collective-permute-start.2 = (f32[2,16,18,1]{3,1,2,0:T(8,128)S(1)}, f32[2,16,18,1]{3,1,2,0:T(8,128)S(1)}, u32[]{:S(2)}, u32[]{:S(2)}) collective-permute-start(f32[2,16,18,1]{3,1,2,0:T(8,128)S(1)} %get-tuple-element.114), channel_id=1, source_target_pairs={{0,1},{1,2},{2,3},{3,4},{4,5},{5,6},{6,7},{7,8},{8,9},{9,10},{10,1... | collective-permute-start | bytes 6920 | tf_op jit(solution)/shard_map/ppermute | solution.py:19
  23.9 11.0 %collective-permute-start.3 = (f32[2,16,18,1]{3,1,2,0:T(8,128)S(1)}, f32[2,16,18,1]{3,1,2,0:T(8,128)S(1)}, u32[]{:S(2)}, u32[]{:S(2)}) collective-permute-start(f32[2,16,18,1]{3,1,2,0:T(8,128)S(1)} %get-tuple-element.115), channel_id=1, source_target_pairs={{1,0},{2,1},{3,2},{4,3},{5,4},{6,5},{7,6},{8,7},{9,8},{10,9},{11,1... | collective-permute-start | bytes 6920 | tf_op jit(solution)/shard_map/ppermute | solution.py:20
  50.2 5.5 %collective-permute-start.5 = (f32[16,1,128]{2,0,1:T(8,128)S(1)}, f32[16,1,128]{2,0,1:T(8,128)S(1)}, u32[]{:S(2)}, u32[]{:S(2)}) collective-permute-start(f32[16,1,128]{2,0,1:T(8,128)S(1)} %get-tuple-element.123), channel_id=1, source_target_pairs={{16,0},{17,1},{18,2},{19,3},{20,4},{21,5},{22,6},{23,7},{24,8},{25... | collective-permute-start | bytes 24584 | tf_op jit(solution)/shard_map/ppermute | solution.py:20
  55.8 7.7 %collective-permute-start.6 = (f32[16,18,1]{2,0,1:T(8,128)S(1)}, f32[16,18,1]{2,0,1:T(8,128)S(1)}, u32[]{:S(2)}, u32[]{:S(2)}) collective-permute-start(f32[16,18,1]{2,0,1:T(8,128)S(1)} %get-tuple-element.120), channel_id=1, source_target_pairs={{0,1},{1,2},{2,3},{3,4},{4,5},{5,6},{6,7},{7,8},{8,9},{9,10},{10,1... | collective-permute-start | bytes 3464 | tf_op jit(solution)/shard_map/ppermute | solution.py:19
  60.7 7.9 %collective-permute-start.7 = (f32[16,18,1]{2,0,1:T(8,128)S(1)}, f32[16,18,1]{2,0,1:T(8,128)S(1)}, u32[]{:S(2)}, u32[]{:S(2)}) collective-permute-start(f32[16,18,1]{2,0,1:T(8,128)S(1)} %get-tuple-element.121), channel_id=1, source_target_pairs={{1,0},{2,1},{3,2},{4,3},{5,4},{6,5},{7,6},{8,7},{9,8},{10,9},{11,1... | collective-permute-start | bytes 3464 | tf_op jit(solution)/shard_map/ppermute | solution.py:20
  84.1 3.1 collective-permute-start.8
  85.8 5.6 %collective-permute-start.9 = (f32[2,16,1,128]{3,1,2,0:T(8,128)S(1)}, f32[2,16,1,128]{3,1,2,0:T(8,128)S(1)}, u32[]{:S(2)}, u32[]{:S(2)}) collective-permute-start(f32[2,16,1,128]{3,1,2,0:T(8,128)S(1)} %get-tuple-element.117), channel_id=1, source_target_pairs={{16,0},{17,1},{18,2},{19,3},{20,4},{21,5},{22,6},{23,7},{24,8},{25... | collective-permute-start | bytes 49160 | tf_op jit(solution)/shard_map/ppermute | solution.py:20
  91.6 7.9 %collective-permute-start.10 = (f32[2,16,18,1]{3,1,2,0:T(8,128)S(1)}, f32[2,16,18,1]{3,1,2,0:T(8,128)S(1)}, u32[]{:S(2)}, u32[]{:S(2)}) collective-permute-start(f32[2,16,18,1]{3,1,2,0:T(8,128)S(1)} %get-tuple-element.112), channel_id=1, source_target_pairs={{0,1},{1,2},{2,3},{3,4},{4,5},{5,6},{6,7},{7,8},{8,9},{9,10},{10,1... | collective-permute-start | bytes 6920 | tf_op jit(solution)/shard_map/ppermute | solution.py:19
  93.1 11.1 %collective-permute-start.11 = (f32[2,16,18,1]{3,1,2,0:T(8,128)S(1)}, f32[2,16,18,1]{3,1,2,0:T(8,128)S(1)}, u32[]{:S(2)}, u32[]{:S(2)}) collective-permute-start(f32[2,16,18,1]{3,1,2,0:T(8,128)S(1)} %get-tuple-element.113), channel_id=1, source_target_pairs={{1,0},{2,1},{3,2},{4,3},{5,4},{6,5},{7,6},{8,7},{9,8},{10,9},{11,1... | collective-permute-start | bytes 6920 | tf_op jit(solution)/shard_map/ppermute | solution.py:20
  115.3 3.7 %collective-permute-start.12 = (f32[3,16,1,128]{3,1,2,0:T(8,128)S(1)}, f32[3,16,1,128]{3,1,2,0:T(8,128)S(1)}, u32[]{:S(2)}, u32[]{:S(2)}) collective-permute-start(f32[3,16,1,128]{3,1,2,0:T(8,128)S(1)} %get-tuple-element.110), channel_id=1, source_target_pairs={{0,16},{1,17},{2,18},{3,19},{4,20},{5,21},{6,22},{7,23},{8,24},{9,... | collective-permute-start | bytes 73736 | tf_op jit(solution)/shard_map/ppermute | solution.py:19
  117.6 5.7 %collective-permute-start.13 = (f32[3,16,1,128]{3,1,2,0:T(8,128)S(1)}, f32[3,16,1,128]{3,1,2,0:T(8,128)S(1)}, u32[]{:S(2)}, u32[]{:S(2)}) collective-permute-start(f32[3,16,1,128]{3,1,2,0:T(8,128)S(1)} %get-tuple-element.111), channel_id=1, source_target_pairs={{16,0},{17,1},{18,2},{19,3},{20,4},{21,5},{22,6},{23,7},{24,8},{25... | collective-permute-start | bytes 73736 | tf_op jit(solution)/shard_map/ppermute | solution.py:20
  123.9 8.2 %collective-permute-start.14 = (f32[3,16,18,1]{2,1,3,0:T(8,128)S(1)}, f32[3,16,18,1]{2,1,3,0:T(8,128)S(1)}, u32[]{:S(2)}, u32[]{:S(2)}) collective-permute-start(f32[3,16,18,1]{2,1,3,0:T(8,128)S(1)} %copy.174), channel_id=1, source_target_pairs={{0,1},{1,2},{2,3},{3,4},{4,5},{5,6},{6,7},{7,8},{8,9},{9,10},{10,1... | collective-permute-start | bytes 10376 | tf_op jit(solution)/shard_map/ppermute | solution.py:19
  130.7 5.8 %collective-permute-start.15 = (f32[3,16,18,1]{2,1,3,0:T(8,128)S(1)}, f32[3,16,18,1]{2,1,3,0:T(8,128)S(1)}, u32[]{:S(2)}, u32[]{:S(2)}) collective-permute-start(f32[3,16,18,1]{2,1,3,0:T(8,128)S(1)} %copy.175), channel_id=1, source_target_pairs={{1,0},{2,1},{3,2},{4,3},{5,4},{6,5},{7,6},{8,7},{9,8},{10,9},{11,1... | collective-permute-start | bytes 10376 | tf_op jit(solution)/shard_map/ppermute | solution.py:20
  191.8 3.4 collective-permute-start.16
  193.7 5.7 %collective-permute-start.17 = (f32[3,16,1,128]{3,1,2,0:T(8,128)S(1)}, f32[3,16,1,128]{3,1,2,0:T(8,128)S(1)}, u32[]{:S(2)}, u32[]{:S(2)}) collective-permute-start(f32[3,16,1,128]{3,1,2,0:T(8,128)S(1)} %get-tuple-element.109), channel_id=1, source_target_pairs={{16,0},{17,1},{18,2},{19,3},{20,4},{21,5},{22,6},{23,7},{24,8},{25... | collective-permute-start | bytes 73736 | tf_op jit(solution)/shard_map/ppermute | solution.py:20
  200.1 5.7 %collective-permute-start.18 = (f32[3,16,18,1]{2,1,3,0:T(8,128)S(1)}, f32[3,16,18,1]{2,1,3,0:T(8,128)S(1)}, u32[]{:S(2)}, u32[]{:S(2)}) collective-permute-start(f32[3,16,18,1]{2,1,3,0:T(8,128)S(1)} %copy.190), channel_id=1, source_target_pairs={{0,1},{1,2},{2,3},{3,4},{4,5},{5,6},{6,7},{7,8},{8,9},{9,10},{10,1... | collective-permute-start | bytes 10376 | tf_op jit(solution)/shard_map/ppermute | solution.py:19
  204.3 5.7 %collective-permute-start.19 = (f32[3,16,18,1]{2,1,3,0:T(8,128)S(1)}, f32[3,16,18,1]{2,1,3,0:T(8,128)S(1)}, u32[]{:S(2)}, u32[]{:S(2)}) collective-permute-start(f32[3,16,18,1]{2,1,3,0:T(8,128)S(1)} %copy.191), channel_id=1, source_target_pairs={{1,0},{2,1},{3,2},{4,3},{5,4},{6,5},{7,6},{8,7},{9,8},{10,9},{11,1... | collective-permute-start | bytes 10376 | tf_op jit(solution)/shard_map/ppermute | solution.py:20
  266.6 3.4 collective-permute-start.20
  268.5 5.7 %collective-permute-start.21 = (f32[3,16,1,128]{3,1,2,0:T(8,128)S(1)}, f32[3,16,1,128]{3,1,2,0:T(8,128)S(1)}, u32[]{:S(2)}, u32[]{:S(2)}) collective-permute-start(f32[3,16,1,128]{3,1,2,0:T(8,128)S(1)} %get-tuple-element.107), channel_id=1, source_target_pairs={{16,0},{17,1},{18,2},{19,3},{20,4},{21,5},{22,6},{23,7},{24,8},{25... | collective-permute-start | bytes 73736 | tf_op jit(solution)/shard_map/ppermute | solution.py:20
  274.8 6.1 %collective-permute-start.22 = (f32[3,16,18,1]{2,1,3,0:T(8,128)S(1)}, f32[3,16,18,1]{2,1,3,0:T(8,128)S(1)}, u32[]{:S(2)}, u32[]{:S(2)}) collective-permute-start(f32[3,16,18,1]{2,1,3,0:T(8,128)S(1)} %copy.192), channel_id=1, source_target_pairs={{0,1},{1,2},{2,3},{3,4},{4,5},{5,6},{6,7},{7,8},{8,9},{9,10},{10,1... | collective-permute-start | bytes 10376 | tf_op jit(solution)/shard_map/ppermute | solution.py:19
  279.4 5.7 %collective-permute-start.23 = (f32[3,16,18,1]{2,1,3,0:T(8,128)S(1)}, f32[3,16,18,1]{2,1,3,0:T(8,128)S(1)}, u32[]{:S(2)}, u32[]{:S(2)}) collective-permute-start(f32[3,16,18,1]{2,1,3,0:T(8,128)S(1)} %copy.193), channel_id=1, source_target_pairs={{1,0},{2,1},{3,2},{4,3},{5,4},{6,5},{7,6},{8,7},{9,8},{10,9},{11,1... | collective-permute-start | bytes 10376 | tf_op jit(solution)/shard_map/ppermute | solution.py:20
  342.3 11.9 %all-to-all-start = ((f32[6,16,16,128]{3,2,0,1:T(8,128)}), f32[6,16,16,128]{3,2,0,1:T(8,128)S(1)}, u32[]{:S(2)}, u32[]{:S(2)}) async-start(f32[6,16,16,128]{3,2,0,1:T(8,128)} %copy.186), calls=%async_computation | async-start | bytes 1572864 | tf_op jit(solution)/shard_map/all_to_all | solution.py:164
  (3 other events, 31.5 us)
